TPU v7x, 512 devices: a whole 4x4x16 slice. The times are simulated.
512 devices in a mesh: gx: 8 (over x, core), gy: 16 (over z), lev: 4 (over y).
Axes of the slice: x: 4, y: 4, z: 16, core: 2. Of those that a mesh axis runs over, the one named last changes fastest.
Arguments:
- zonal: float32 [128, 256, 2048], P('lev', 'gx', 'gy'), may hold values from -6 to 6
- meridional: float32 [128, 256, 2048], P('lev', 'gx', 'gy'), may hold values from -6 to 6
- vertical: float32 [128, 256, 2048], P('lev', 'gx', 'gy'), may hold values from -4 to 4
- pressure: float32 [128, 256, 2048], P('lev', 'gx', 'gy'), may hold values from -6 to 6
- coupling: float32 [128, 256, 2048], P('lev', 'gx', 'gy'), may hold values from 0.125 to 32768
- surface: int32 [256, 2048], P('gx', 'gy'), may hold values from 0 to 16
- lid_flag: int32 [256, 2048], P('gx', 'gy'), may hold values from 0 to 1
Outputs:
- zonal_out: float32 [128, 256, 2048], P('lev', 'gx', 'gy')
- meridional_out: float32 [128, 256, 2048], P('lev', 'gx', 'gy')
- vertical_out: float32 [128, 256, 2048], P('lev', 'gx', 'gy')
- pressure_out: float32 [128, 256, 2048], P('lev', 'gx', 'gy')
Inputs may be any that keep to these rules, and one draw needn't show every extreme that they name: `surface`: the number of lowest levels of a column that lie below the terrain. `lid_flag`: 1 closes the column's top with a rigid lid, 0 leaves it open.
All inputs are finite; a program needn't handle non-finite values.
Results may differ from a plain program's by a relative error of at most 0.0003.
Values sent between devices are 32-bit elements; how exact they have to be, the bound alone decides.
A program may use at most 128 MiB of HBM per device.

v0:
```python
import functools

import jax
import jax.numpy as jnp
from jax import lax
from jax.experimental import pallas as pl
from jax.experimental.pallas import tpu as pltpu
from jax.sharding import PartitionSpec as P

SUBSTEPS = 3
MESH = pl.DeviceIdType.MESH
PAD = 8


def kernel(
    zon, mer, ver, pre, cou, sur, lid,
    out_u, out_v, out_w, out_p,
    us, vs, ws, ps, cs, ks, ls,
    fs, pp, zz, am, im, gm, gf, gl,
    xs0, ys0, xs, ys, xr0, yr0, xr, yr,
    sta, lev, cup, pls, plr, inv,
    load_sem, store_sem, send_sem, recv_sem,
):
    L, I, J = zon.shape
    g = lax.axis_index("lev")
    gx = lax.axis_index("gx")
    gy = lax.axis_index("gy")
    groups = lax.axis_size("lev")
    nx = lax.axis_size("gx")
    ny = lax.axis_size("gy")
    x_lo = {"gx": lax.rem(gx + nx - 1, nx)}
    x_hi = {"gx": lax.rem(gx + 1, nx)}
    y_lo = {"gy": lax.rem(gy + ny - 1, ny)}
    y_hi = {"gy": lax.rem(gy + 1, ny)}
    peers = [{"lev": lax.rem(g + d, groups)} for d in range(1, groups)]
    inner = pl.ds(PAD, I)

    loads = [
        pltpu.make_async_copy(src, dst, load_sem.at[n])
        for n, (src, dst) in enumerate([
            (pre, ps.at[:, inner, :]),
            (mer, vs),
            (zon, us.at[:, inner, :]),
            (cou, cs.at[pl.ds(0, L)]),
            (sur, ks),
            (lid, ls),
            (ver, ws),
        ])
    ]
    for copy in loads:
        copy.start()
    barrier = pltpu.get_barrier_semaphore()
    everyone = [x_lo, x_hi, y_lo, y_hi] + peers
    for dev in everyone:
        pl.semaphore_signal(barrier, inc=1, device_id=dev, device_id_type=MESH)

    lane = lax.broadcasted_iota(jnp.int32, (I, J), 1)
    quad = lane // 4
    sub = lane % 4
    edge = (lane < 2) | (lane >= J - 2)
    zero = jnp.zeros((I, J), jnp.float32)

    def rows_out(src2, buf, side, at, row):
        buf[side, pl.ds(at * L, L), :] = src2[:, PAD + row, :]

    def rows_in(dst2, row, buf, side, at):
        dst2[:, PAD + row, :] = buf[side, pl.ds(at * L, L), :]

    sems = iter(range(64))

    def remote(src, dst, dev):
        n = next(sems)
        return pltpu.make_async_remote_copy(
            src_ref=src, dst_ref=dst, send_sem=send_sem.at[n], recv_sem=recv_sem.at[n],
            device_id=dev, device_id_type=MESH)

    loads[0].wait()
    loads[1].wait()
    loads[2].wait()
    for r in range(2):
        rows_out(ps, xs0, 0, r, r)
        rows_out(ps, xs0, 1, r, I - 2 + r)
    rows_out(us, xs0, 0, 2, 0)
    rows_out(us, xs0, 1, 2, I - 1)

    def pack0(k, held):
        a, b = held
        turn = 4 * k + 2
        mine = quad == k
        a = jnp.where(mine, pltpu.roll(ps[k, inner, :], turn, 1), a)
        b = jnp.where(mine, pltpu.roll(vs[k], turn, 1), b)
        return a, b

    pack, pack_v = lax.fori_loop(0, L, pack0, (zero, zero), unroll=8)
    ys0[0] = pack
    ys0[1] = pack_v
    for n in range(3, 6):
        loads[n].wait()

    pl.semaphore_wait(barrier, len(everyone))
    first = [
        remote(xs0.at[0], xr0.at[1], x_lo),
        remote(xs0.at[1], xr0.at[0], x_hi),
        remote(ys0, yr0.at[1], y_lo),
        remote(ys0, yr0.at[0], y_hi),
        remote(cs.at[0], cup, peers[-1]),
    ]
    for copy in first:
        copy.start()

    cs[L] = zero
    height = ks[...] - g * L
    lid_here = jnp.where(g == groups - 1, ls[...].astype(jnp.float32), 0.0)
    start = jnp.where(g == 0, 1.0, 0.0).astype(jnp.float32)

    def factor(k, held):
        rate, z = held
        here = cs[k]
        above = cs[k + 1]
        keep = height <= k
        delta = 1.0 + here * rate + jnp.where(k == L - 1, lid_here * here, 0.0)
        one = 1.0 / (delta + above)
        rate = jnp.where(keep, delta * one, 1.0)
        one = jnp.where(keep, one, 0.0)
        a = here * one
        z = jnp.where(k == 0, one, a * z)
        im[k] = one
        am[k] = a
        gm[k] = above * one
        gf[k] = z
        return rate, z

    lax.fori_loop(0, L, factor, (zero + start, zero), unroll=4)

    def respond(n, held):
        a, b = held
        k = L - 1 - n
        up = gm[k]
        a = gf[k] + up * a
        b = jnp.where(n == 0, im[L - 1], up * b)
        gf[k] = a
        gl[k] = b
        return a, b

    lax.fori_loop(0, L, respond, (zero, zero), unroll=4)
    own_inv = 1.0 / cs[0]
    sta[g, 0] = gf[0] + own_inv
    sta[g, 1] = gf[L - 1]
    sta[g, 2] = gl[L - 1]
    spread = [remote(sta.at[g], sta.at[g], dev) for dev in peers]
    for copy in spread:
        copy.start()
    loads[6].wait()

    below_sign = jnp.where(g == 0, 0.0, -1.0).astype(jnp.float32)
    above_sign = jnp.where(g == groups - 1, 0.0, -1.0).astype(jnp.float32)
    has_below = jnp.where(g == 0, 0.0, 1.0).astype(jnp.float32)
    up_inv = zero
    pending = []

    for step in range(SUBSTEPS):
        if step == 0:
            for copy in first:
                copy.wait_recv()
            for r in range(2):
                rows_in(ps, r - 2, xr0, 0, r)
                rows_in(ps, I + r, xr0, 1, r)
            rows_in(us, -1, xr0, 0, 2)
            rows_in(us, I, xr0, 1, 2)
            from_lo, from_hi = yr0[0, 0], yr0[1, 0]
            side_lo, side_hi = yr0[0, 1] - pack_v, yr0[1, 1] - pack_v
            spin = jnp.where(sub == 1, pltpu.roll(side_hi, J - 1, 1),
                             jnp.where(sub == 2, -pltpu.roll(side_lo, 1, 1), 0.0))
            up_inv = 1.0 / cup[...]
        else:
            for copy in halo:
                copy.wait_recv()
            n = step - 1
            for r in range(2):
                rows_in(ps, r - 2, xr.at[n], 0, r)
                rows_in(ps, I + r, xr.at[n], 1, r)
            from_lo, from_hi = yr[n, 0], yr[n, 1]
        from_lo = from_lo - pack
        from_hi = from_hi - pack
        mend2 = 0.0625 * jnp.where(sub < 2, pltpu.roll(from_hi, J - 2, 1), pltpu.roll(from_lo, 2, 1))
        mend1 = jnp.where(sub == 1, pltpu.roll(from_hi, J - 1, 1),
                          jnp.where(sub == 2, -pltpu.roll(from_lo, 1, 1), 0.0))
        if step == 0:
            mend2 = mend2 - 0.25 * spin

        def predict(k, _):
            here = ps[k, inner, :]
            fix = jnp.where(edge, pltpu.roll(mend2, J - 2 - 4 * k, 1), 0.0)
            lap = (ps[k, pl.ds(PAD + 2, I), :] + ps[k, pl.ds(PAD - 2, I), :]
                   + pltpu.roll(here, J - 2, 1) + pltpu.roll(here, 2, 1) - 4.0 * here)
            force = 0.0625 * lap + fix
            if step == 0:
                v = vs[k]
                spr = (us[k, pl.ds(PAD + 1, I), :] - us[k, pl.ds(PAD - 1, I), :]
                       + pltpu.roll(v, J - 1, 1) - pltpu.roll(v, 1, 1))
                force = force - 0.25 * spr
            else:
                force = force + fs[k]
            fs[k] = force
            pp[k + 1] = here + force
            return 0

        lax.fori_loop(0, L, predict, 0, unroll=4)
        low = pp[1]
        top = pp[L]
        pp[0] = below_sign * low
        pp[L + 1] = above_sign * top

        def forward(k, z):
            one = im[k]
            z = (ws[k] - 0.5 * (pp[k + 2] - pp[k])) * one + am[k] * z
            zz[k] = z
            return z

        lax.fori_loop(0, L, forward, zero, unroll=4)

        def backward(n, y):
            k = L - 1 - n
            y = zz[k] + gm[k] * y
            zz[k] = y
            return y

        lax.fori_loop(0, L, backward, zero, unroll=4)
        lev[step, g, 0] = zz[0] - 0.5 * low * own_inv
        lev[step, g, 1] = zz[L - 1] + 0.5 * top * up_inv
        pls[step] = top
        around = [remote(lev.at[step, g], lev.at[step, g], dev) for dev in peers]
        around.append(remote(pls.at[step], plr.at[step], peers[0]))
        for copy in around:
            copy.start()

        def move(k, _):
            here = ps[k, inner, :]
            fix = jnp.where(edge, pltpu.roll(mend1, J - 2 - 4 * k, 1), 0.0)
            us[k, inner, :] = us[k, inner, :] - 0.25 * (
                ps[k, pl.ds(PAD + 1, I), :] - ps[k, pl.ds(PAD - 1, I), :])
            vs[k] = vs[k] - 0.25 * (
                pltpu.roll(here, J - 1, 1) - pltpu.roll(here, 1, 1) + fix)
            return 0

        lax.fori_loop(0, L, move, 0, unroll=4)
        if step == SUBSTEPS - 1:
            stores = [
                pltpu.make_async_copy(us.at[:, inner, :], out_u, store_sem.at[0]),
                pltpu.make_async_copy(vs, out_v, store_sem.at[1]),
            ]
            for copy in stores:
                copy.start()

        if step == 0:
            for copy in spread:
                copy.wait_recv()
            d1 = sta[1, 0] + sta[0, 2]
            d2 = sta[2, 0] + sta[1, 2]
            d3 = sta[3, 0] + sta[2, 2]
            q1 = sta[1, 1]
            q2 = sta[2, 1]
            m1 = d2 * d3 - q2 * q2
            whole = 1.0 / (d1 * m1 - q1 * q1 * d3)
            n11 = m1 * whole
            n12 = q1 * d3 * whole
            n13 = q1 * q2 * whole
            n22 = d1 * d3 * whole
            n23 = d1 * q2 * whole
            n33 = (d1 * d2 - q1 * q1) * whole
            for slot, face in ((0, g), (1, g + 1)):
                for col, three in enumerate(((n11, n12, n13), (n12, n22, n23), (n13, n23, n33))):
                    inv[slot, col] = jnp.where(face == 1, three[0], jnp.where(
                        face == 2, three[1], jnp.where(face == 3, three[2], 0.0)))

        for copy in around:
            copy.wait_recv()
        r1 = lev[step, 1, 0] - lev[step, 0, 1]
        r2 = lev[step, 2, 0] - lev[step, 1, 1]
        r3 = lev[step, 3, 0] - lev[step, 2, 1]
        under = inv[0, 0] * r1 + inv[0, 1] * r2 + inv[0, 2] * r3
        over = inv[1, 0] * r1 + inv[1, 1] * r2 + inv[1, 2] * r3
        jump = (under + 0.5 * (low + plr[step])) * own_inv

        def correct(k, held):
            before, acc = held
            x = zz[k] - gf[k] * under + gl[k] * over
            before = jnp.where(k == 0, has_below * (x - jump), before)
            new = pp[k + 1] - 0.5 * (x - before)
            ws[k] = x
            ps[k, inner, :] = new
            if step < SUBSTEPS - 1:
                acc = jnp.where(quad == k, pltpu.roll(new, 4 * k + 2, 1), acc)
            return x, acc

        unused, pack = lax.fori_loop(0, L, correct, (zero, zero), unroll=4)
        pending += around
        if step < SUBSTEPS - 1:
            for r in range(2):
                rows_out(ps, xs.at[step], 0, r, r)
                rows_out(ps, xs.at[step], 1, r, I - 2 + r)
            ys[step] = pack
            halo = [
                remote(xs.at[step, 0], xr.at[step, 1], x_lo),
                remote(xs.at[step, 1], xr.at[step, 0], x_hi),
                remote(ys.at[step], yr.at[step, 1], y_lo),
                remote(ys.at[step], yr.at[step, 0], y_hi),
            ]
            for copy in halo:
                copy.start()
            pending += halo

    stores += [
        pltpu.make_async_copy(ws, out_w, store_sem.at[2]),
        pltpu.make_async_copy(ps.at[:, inner, :], out_p, store_sem.at[3]),
    ]
    for copy in stores[2:]:
        copy.start()
    for copy in first + spread + pending:
        copy.wait_send()
    for copy in stores:
        copy.wait()


def body(zonal, meridional, vertical, pressure, coupling, surface, lid_flag):
    L, I, J = zonal.shape
    IP = I + 2 * PAD
    f32 = jnp.float32
    V = lambda *shape: pltpu.VMEM(shape, f32)
    n_sem = 5 + 3 + 4 * SUBSTEPS + 4 * (SUBSTEPS - 1)
    any_spec = pl.BlockSpec(memory_space=pl.ANY)
    field = jax.ShapeDtypeStruct((L, I, J), f32)
    S = SUBSTEPS
    return tuple(pl.pallas_call(
        kernel,
        out_shape=(field,) * 4,
        in_specs=[any_spec] * 7,
        out_specs=(any_spec,) * 4,
        scratch_shapes=[
            V(L, IP, J), V(L, I, J), V(L, I, J), V(L, IP, J), V(L + 1, I, J),
            pltpu.VMEM((I, J), jnp.int32), pltpu.VMEM((I, J), jnp.int32),
            V(L, I, J), V(L + 2, I, J), V(L, I, J), V(L, I, J), V(L, I, J), V(L, I, J),
            V(L, I, J), V(L, I, J),
            V(2, 3 * L, J), V(2, I, J), V(S - 1, 2, 2 * L, J), V(S - 1, I, J),
            V(2, 3 * L, J), V(2, 2, I, J), V(S - 1, 2, 2 * L, J), V(S - 1, 2, I, J),
            V(4, 3, I, J), V(S, 4, 2, I, J), V(I, J), V(S, I, J), V(S, I, J), V(2, 3, I, J),
            pltpu.SemaphoreType.DMA((7,)),
            pltpu.SemaphoreType.DMA((4,)),
            pltpu.SemaphoreType.DMA((n_sem,)),
            pltpu.SemaphoreType.DMA((n_sem,)),
        ],
        compiler_params=pltpu.CompilerParams(collective_id=0, has_side_effects=True),
    )(zonal, meridional, vertical, pressure, coupling, surface, lid_flag))


def solution(mesh):
    field = P("lev", "gx", "gy")
    plane = P("gx", "gy")
    return jax.shard_map(
        body, mesh=mesh,
        in_specs=(field,) * 5 + (plane,) * 2,
        out_specs=(field,) * 4,
        check_vma=False,
    )
```

profile of v0, /device:TPU:1, one launch (start us, length us, event | category | flops | bytes accessed | tf_op | source)
XLA Modules:
  0.0 48.9 jit_solution(9810677483566605245)
XLA Ops:
  0.6 43.1 %shard_map.102 = (f32[32,32,128]{2,1,0:T(8,128)}, f32[32,32,128]{2,1,0:T(8,128)}, f32[32,32,128]{2,1,0:T(8,128)}, f32[32,32,128]{2,1,0:T(8,128)}) custom-call(f32[32,32,128]{2,1,0:T(8,128)} %zon.1, f32[32,32,128]{2,1,0:T(8,128)} %mer.1, f32[32,32,128]{2,1,0:T(8,128)} %ver.1, f32[32,32,128]{2,1,0:T(8,128)} %pre.1, f32[32,32,128]{2,1,0:T(8,128)} %cou.1, ...), custom_call_target="tpu_custom_call" | custom-call | tf_op jit(solution)/shard_map/pallas_call | solution.py:334
  43.7 0.0 copy-start.2
  43.7 1.9 %copy.15 = f32[32,32,128]{2,1,0:T(8,128)} copy(f32[32,32,128]{2,1,0:T(8,128)} %get-tuple-element.8) | data formatting | bytes 1048576
  45.7 0.0 copy-done.2
  45.7 0.0 copy-start.1
  45.7 0.8 %copy.16 = f32[32,32,128]{2,1,0:T(8,128)} copy(f32[32,32,128]{2,1,0:T(8,128)S(1)} %copy-done.2) | data formatting | bytes 1048576
  46.5 0.4 copy-done.1
  46.9 0.0 copy-start
  46.9 0.8 %copy.17 = f32[32,32,128]{2,1,0:T(8,128)} copy(f32[32,32,128]{2,1,0:T(8,128)S(1)} %copy-done.1) | data formatting | bytes 1048576
  47.7 0.4 copy-done
  48.1 0.8 %copy.18 = f32[32,32,128]{2,1,0:T(8,128)} copy(f32[32,32,128]{2,1,0:T(8,128)S(1)} %copy-done) | data formatting | bytes 1048576
Async XLA Ops:
  43.7 1.9 %copy-start.2 = (f32[32,32,128]{2,1,0:T(8,128)S(1)}, f32[32,32,128]{2,1,0:T(8,128)}, u32[]{:S(2)}) copy-start(f32[32,32,128]{2,1,0:T(8,128)} %get-tuple-element.9) | copy-start | bytes 1572868
  45.7 1.2 %copy-start.1 = (f32[32,32,128]{2,1,0:T(8,128)S(1)}, f32[32,32,128]{2,1,0:T(8,128)}, u32[]{:S(2)}) copy-start(f32[32,32,128]{2,1,0:T(8,128)} %get-tuple-element.10) | copy-start | bytes 1572868
  46.9 1.2 %copy-start = (f32[32,32,128]{2,1,0:T(8,128)S(1)}, f32[32,32,128]{2,1,0:T(8,128)}, u32[]{:S(2)}) copy-start(f32[32,32,128]{2,1,0:T(8,128)} %get-tuple-element.11) | copy-start | bytes 1572868
where the time goes:
time: 49.2 us; the launch traced here: 48.9 us
  Pallas kernels  43.1 us (88%)
  local copies, waits for them, and re-layouts  5.18 us (11%)
  between operations  0.65 us (1%)
    pallas_call x1, Pallas kernels, body(): pl.pallas_call(kernel, out_shape=(field,) * 4, in_specs=[any_spec] * 7, o...  43.1 us
    unnamed x10, local copies, waits for them, and re-layouts  5.18 us

commit v1 on v0

--- a/solution.py
+++ b/solution.py
@@ -19,7 +19,7 @@
     fs, pp, zz, am, im, gm, gf, gl,
     xs0, ys0, xs, ys, xr0, yr0, xr, yr,
     sta, lev, cup, pls, plr, inv,
-    load_sem, store_sem, send_sem, recv_sem,
+    load_sem, send_sem, recv_sem,
 ):
     L, I, J = zon.shape
     g = lax.axis_index("lev")
@@ -159,6 +159,7 @@
     pending = []
 
     for step in range(SUBSTEPS):
+        last = step == SUBSTEPS - 1
         if step == 0:
             for copy in first:
                 copy.wait_recv()
@@ -237,21 +238,19 @@
         def move(k, _):
             here = ps[k, inner, :]
             fix = jnp.where(edge, pltpu.roll(mend1, J - 2 - 4 * k, 1), 0.0)
-            us[k, inner, :] = us[k, inner, :] - 0.25 * (
+            new_u = us[k, inner, :] - 0.25 * (
                 ps[k, pl.ds(PAD + 1, I), :] - ps[k, pl.ds(PAD - 1, I), :])
-            vs[k] = vs[k] - 0.25 * (
+            new_v = vs[k] - 0.25 * (
                 pltpu.roll(here, J - 1, 1) - pltpu.roll(here, 1, 1) + fix)
+            if last:
+                out_u[k] = new_u
+                out_v[k] = new_v
+            else:
+                us[k, inner, :] = new_u
+                vs[k] = new_v
             return 0
 
         lax.fori_loop(0, L, move, 0, unroll=4)
-        if step == SUBSTEPS - 1:
-            stores = [
-                pltpu.make_async_copy(us.at[:, inner, :], out_u, store_sem.at[0]),
-                pltpu.make_async_copy(vs, out_v, store_sem.at[1]),
-            ]
-            for copy in stores:
-                copy.start()
-
         if step == 0:
             for copy in spread:
                 copy.wait_recv()
@@ -287,15 +286,18 @@
             x = zz[k] - gf[k] * under + gl[k] * over
             before = jnp.where(k == 0, has_below * (x - jump), before)
             new = pp[k + 1] - 0.5 * (x - before)
-            ws[k] = x
-            ps[k, inner, :] = new
-            if step < SUBSTEPS - 1:
+            if last:
+                out_w[k] = x
+                out_p[k] = new
+            else:
+                ws[k] = x
+                ps[k, inner, :] = new
                 acc = jnp.where(quad == k, pltpu.roll(new, 4 * k + 2, 1), acc)
             return x, acc
 
         unused, pack = lax.fori_loop(0, L, correct, (zero, zero), unroll=4)
         pending += around
-        if step < SUBSTEPS - 1:
+        if not last:
             for r in range(2):
                 rows_out(ps, xs.at[step], 0, r, r)
                 rows_out(ps, xs.at[step], 1, r, I - 2 + r)
@@ -310,15 +312,18 @@
                 copy.start()
             pending += halo
 
-    stores += [
-        pltpu.make_async_copy(ws, out_w, store_sem.at[2]),
-        pltpu.make_async_copy(ps.at[:, inner, :], out_p, store_sem.at[3]),
-    ]
-    for copy in stores[2:]:
-        copy.start()
     for copy in first + spread + pending:
         copy.wait_send()
-    for copy in stores:
+
+
+def store_kernel(*refs):
+    sem = refs[-1]
+    copies = [
+        pltpu.make_async_copy(refs[n], refs[4 + n], sem.at[n]) for n in range(4)
+    ]
+    for copy in copies:
+        copy.start()
+    for copy in copies:
         copy.wait()
 
 
@@ -331,11 +336,12 @@
     any_spec = pl.BlockSpec(memory_space=pl.ANY)
     field = jax.ShapeDtypeStruct((L, I, J), f32)
     S = SUBSTEPS
-    return tuple(pl.pallas_call(
+    vmem_spec = pl.BlockSpec(memory_space=pltpu.VMEM)
+    results = pl.pallas_call(
         kernel,
-        out_shape=(field,) * 4,
+        out_shape=(V(L, I, J),) * 4,
         in_specs=[any_spec] * 7,
-        out_specs=(any_spec,) * 4,
+        out_specs=(vmem_spec,) * 4,
         scratch_shapes=[
             V(L, IP, J), V(L, I, J), V(L, I, J), V(L, IP, J), V(L + 1, I, J),
             pltpu.VMEM((I, J), jnp.int32), pltpu.VMEM((I, J), jnp.int32),
@@ -345,12 +351,19 @@
             V(2, 3 * L, J), V(2, 2, I, J), V(S - 1, 2, 2 * L, J), V(S - 1, 2, I, J),
             V(4, 3, I, J), V(S, 4, 2, I, J), V(I, J), V(S, I, J), V(S, I, J), V(2, 3, I, J),
             pltpu.SemaphoreType.DMA((7,)),
-            pltpu.SemaphoreType.DMA((4,)),
             pltpu.SemaphoreType.DMA((n_sem,)),
             pltpu.SemaphoreType.DMA((n_sem,)),
         ],
         compiler_params=pltpu.CompilerParams(collective_id=0, has_side_effects=True),
-    )(zonal, meridional, vertical, pressure, coupling, surface, lid_flag))
+    )(zonal, meridional, vertical, pressure, coupling, surface, lid_flag)
+    return tuple(pl.pallas_call(
+        store_kernel,
+        out_shape=(field,) * 4,
+        in_specs=[vmem_spec] * 4,
+        out_specs=(any_spec,) * 4,
+        scratch_shapes=[pltpu.SemaphoreType.DMA((4,))],
+        compiler_params=pltpu.CompilerParams(vmem_limit_bytes=1 << 22),
+    )(*results))
 
 
 def solution(mesh):

time: 49.2 us -> 44.2 us (0.90)
  local copies, waits for them, and re-layouts: 5.18 us -> 0 us
    unnamed x10 -> x0, local copies, waits for them, and re-layouts: 5.18 us -> none
    pallas_call x1 -> x2, Pallas kernels: 43.1 us -> 43.4 us  [the longest x1 42.1 us: body(): pl.pallas_call(kernel, out_shape=(V(L, I, J),) * 4, in_specs=[any_spec] *...]
where the time goes in v1:
time: 44.2 us; the launch traced here: 44.1 us
  Pallas kernels  43.4 us (98%)
  between operations  0.64 us (1%)
    pallas_call x1, Pallas kernels, body(): pl.pallas_call(kernel, out_shape=(V(L, I, J),) * 4, in_specs=[any_spec] *...  42.1 us
    pallas_call x1, Pallas kernels, body(): pl.pallas_call(store_kernel, out_shape=(field,) * 4, in_specs=[vmem_spec]...  1.35 us

profile of v1, /device:TPU:1, one launch (start us, length us, event | category | flops | bytes accessed | tf_op | source)
XLA Modules:
  0.0 44.1 jit_solution(14523769743705817842)
XLA Ops:
  0.6 42.1 %shard_map.102 = (f32[32,32,128]{2,1,0:T(8,128)S(1)}, f32[32,32,128]{2,1,0:T(8,128)S(1)}, f32[32,32,128]{2,1,0:T(8,128)S(1)}, f32[32,32,128]{2,1,0:T(8,128)S(1)}) custom-call(f32[32,32,128]{2,1,0:T(8,128)} %zon.1, f32[32,32,128]{2,1,0:T(8,128)} %mer.1, f32[32,32,128]{2,1,0:T(8,128)} %ver.1, f32[32,32,128]{2,1,0:T(8,128)} %pre.1, f32[32,32,128]{2,1,0:T(8,128)} %cou.1, ...), custom_call_target="tpu_custom_call" | custom-call | tf_op jit(solution)/shard_map/pallas_call | solution.py:340
  42.7 1.3 %shard_map.103 = (f32[32,32,128]{2,1,0:T(8,128)}, f32[32,32,128]{2,1,0:T(8,128)}, f32[32,32,128]{2,1,0:T(8,128)}, f32[32,32,128]{2,1,0:T(8,128)}) custom-call(f32[32,32,128]{2,1,0:T(8,128)S(1)} %get-tuple-element.8.refs_0_, f32[32,32,128]{2,1,0:T(8,128)S(1)} %get-tuple-element.9.refs_1_, f32[32,32,128]{2,1,0:T(8,128)S(1)} %get-tuple-element.10.refs_2_, ...), custom_call_target="tpu_custom_call" | custom-call | tf_op jit(solution)/shard_map/pallas_call | solution.py:359

commit v2 on v1

v2 whole, which is shorter than its diff:
```python
import functools
import types

import jax
import jax.numpy as jnp
from jax import lax
from jax.experimental import pallas as pl
from jax.experimental.pallas import tpu as pltpu
from jax.sharding import PartitionSpec as P

SUBSTEPS = 3
MESH = pl.DeviceIdType.MESH
PAD = 8
GROUPS = 4


def inverse(d1, d2, d3, q1, q2):
    m1 = d2 * d3 - q2 * q2
    whole = 1.0 / (d1 * m1 - q1 * q1 * d3)
    n12 = q1 * d3 * whole
    n13 = q1 * q2 * whole
    n23 = d1 * q2 * whole
    return (
        (m1 * whole, n12, n13),
        (n12, d1 * d3 * whole, n23),
        (n13, n23, (d1 * d2 - q1 * q1) * whole),
    )


def face_row(rows, col, face):
    return jnp.where(face == 1, rows[0][col], jnp.where(
        face == 2, rows[1][col], jnp.where(face == 3, rows[2][col], 0.0)))


def kernel(names, zon, mer, ver, pre, cou, sur, lid, out_u, out_v, out_w, out_p, *scratch):
    m = types.SimpleNamespace(**dict(zip(names, scratch)))
    us, vs, ws, ps, cs = m.us, m.vs, m.ws, m.ps, m.cs
    L, I, J = zon.shape
    g = lax.axis_index("lev")
    gx = lax.axis_index("gx")
    gy = lax.axis_index("gy")
    nx = lax.axis_size("gx")
    ny = lax.axis_size("gy")
    groups = GROUPS
    x_dev = ({"gx": lax.rem(gx + nx - 1, nx)}, {"gx": lax.rem(gx + 1, nx)})
    y_dev = ({"gy": lax.rem(gy + ny - 1, ny)}, {"gy": lax.rem(gy + 1, ny)})
    peers = [{"lev": lax.rem(g + d, groups)} for d in range(1, groups)]
    around = [{**dev, "lev": lax.rem(g + d, groups)}
              for d in range(groups) for dev in x_dev + y_dev]
    inner = pl.ds(PAD, I)

    loads = [
        pltpu.make_async_copy(src, dst, m.load_sem.at[n])
        for n, (src, dst) in enumerate([
            (pre, ps.at[:, inner, :]),
            (mer, vs),
            (zon, us.at[:, inner, :]),
            (cou, cs.at[pl.ds(0, L)]),
            (sur, m.ks),
            (lid, m.ls),
            (ver, ws),
        ])
    ]
    for copy in loads:
        copy.start()
    barrier = pltpu.get_barrier_semaphore()
    everyone = peers + around
    for dev in everyone:
        pl.semaphore_signal(barrier, inc=1, device_id=dev, device_id_type=MESH)

    lane = lax.broadcasted_iota(jnp.int32, (I, J), 1)
    level = lax.broadcasted_iota(jnp.int32, (L, J), 0)
    quad = lane // 4
    sub = lane % 4
    edge = (lane < 2) | (lane >= J - 2)
    lane8 = lax.broadcasted_iota(jnp.int32, (8, J), 1)
    quad8 = lane8 // 4
    left8 = lane8 % 4 < 2
    live8 = (quad8 % 4 == 0) & (quad8 < 16)
    zero = jnp.zeros((I, J), jnp.float32)
    halo_rows = jnp.zeros((L, PAD, J), jnp.float32)
    for ref in (ps, us):
        ref[:, 0:PAD, :] = halo_rows
        ref[:, PAD + I:, :] = halo_rows
    pick = lax.broadcasted_iota(jnp.int32, (J, 4 * J), 0)
    into = lax.broadcasted_iota(jnp.int32, (J, 4 * J), 1)
    m.sel[...] = jnp.where(
        (pick % 16 == into % 4) & (pick // 16 == into // J), 1.0, 0.0).astype(jnp.float32)

    counter = iter(range(1 << 10))

    def remote(src, dst, dev):
        n = next(counter)
        return pltpu.make_async_remote_copy(
            src_ref=src, dst_ref=dst, send_sem=m.send_sem.at[n], recv_sem=m.recv_sem.at[n],
            device_id=dev, device_id_type=MESH)

    sent = []

    def start(copies):
        for copy in copies:
            copy.start()
        sent.extend(copies)
        return copies

    def arrive(copies):
        for copy in copies:
            copy.wait_recv()

    def side_row(side, r):
        return r if side == 0 else I - 2 + r

    def packed(k, plane, held):
        return jnp.where(quad == k, pltpu.roll(plane, 4 * k + 2, 1), held)

    def strips(phase, planes):
        tile = jnp.zeros((8, J), jnp.float32)
        for n, plane in enumerate(planes):
            m.xsi[phase, 0, pl.ds(2 * n, 2), :] = plane[0:2]
            m.xsi[phase, 1, pl.ds(2 * n, 2), :] = plane[I - 2:I]
            for v in range(4):
                turned = pltpu.roll(plane[8 * v:8 * v + 8], 16 * v + 4 * n + 2, 1)
                tile = jnp.where(quad8 == 4 * v + n, turned, tile)
        m.ysi[phase] = tile
        return start([
            copy
            for d in range(groups) for side in range(2)
            for copy in (
                remote(m.xsi.at[phase, side], m.xri.at[phase, 1 - side, g], around[4 * d + side]),
                remote(m.ysi.at[phase], m.yri.at[phase, 1 - side, g], around[4 * d + 2 + side]),
            )
        ])

    def x_rows(phase, side, h, n):
        return m.xri[phase, side, h, pl.ds(2 * n, 2), :]

    def y_tile(phase, h):
        return jnp.where(left8, m.yri[phase, 0, h], m.yri[phase, 1, h])

    def turn8(tile, n):
        return pltpu.roll(tile, J - 4 * n, 1) if n else tile

    loads[0].wait()
    loads[1].wait()
    loads[2].wait()
    for side in range(2):
        for r in range(2):
            m.xs0[side, pl.ds(r * L, L), :] = ps[:, PAD + side_row(side, r), :]
        m.xs0[side, pl.ds(2 * L, L), :] = us[:, PAD + (I - 1) * side, :]

    def pack0(k, held):
        return packed(k, ps[k, inner, :], held[0]), packed(k, vs[k], held[1])

    pack, pack_v = lax.fori_loop(0, L, pack0, (zero, zero), unroll=16)
    m.ys0[0] = pack
    m.ys0[1] = pack_v
    for n in range(3, 6):
        loads[n].wait()

    pl.semaphore_wait(barrier, len(everyone))
    first = start([
        remote(m.xs0.at[0], m.xr0.at[1], x_dev[0]),
        remote(m.xs0.at[1], m.xr0.at[0], x_dev[1]),
        remote(m.ys0, m.yr0.at[1], y_dev[0]),
        remote(m.ys0, m.yr0.at[0], y_dev[1]),
        remote(cs.at[0], m.cup, peers[-1]),
    ])

    cs[L] = zero
    height = m.ks[...] - g * L
    lid_here = jnp.where(g == groups - 1, m.ls[...].astype(jnp.float32), 0.0)
    is_first = jnp.where(g == 0, 1.0, 0.0).astype(jnp.float32)
    above_sign = jnp.where(g == groups - 1, 0.0, -1.0).astype(jnp.float32)
    g_below = lax.rem(g + groups - 1, groups)

    def factor(k, held):
        rate, z = held
        here = cs[k]
        above = cs[k + 1]
        keep = height <= k
        delta = 1.0 + here * rate + jnp.where(k == L - 1, lid_here * here, 0.0)
        one = 1.0 / (delta + above)
        rate = jnp.where(keep, delta * one, 1.0)
        one = jnp.where(keep, one, 0.0)
        a = here * one
        z = jnp.where(k == 0, one, a * z)
        m.im[k] = one
        m.am[k] = a
        m.gm[k] = above * one
        m.gf[k] = z
        return rate, z

    lax.fori_loop(0, L, factor, (zero + is_first, zero), unroll=4)

    def respond(n, held):
        a, b = held
        k = L - 1 - n
        up = m.gm[k]
        a = m.gf[k] + up * a
        b = jnp.where(n == 0, m.im[L - 1], up * b)
        m.gf[k] = a
        m.gl[k] = b
        return a, b

    lax.fori_loop(0, L, respond, (zero, zero), unroll=4)
    own_inv = 1.0 / cs[0]
    own_static = (m.gf[0] + own_inv, m.gf[L - 1], m.gl[L - 1])
    for n in range(3):
        m.sta[g, n] = own_static[n]
    static = start([remote(m.sta.at[g], m.sta.at[g], dev) for dev in peers])
    spare = jnp.zeros((2, J), jnp.float32)
    for phase in range(SUBSTEPS):
        for side in range(2):
            m.xsi[phase, side, pl.ds(6, 2), :] = spare
    static += strips(0, own_static)

    def slopes(k, held):
        f_before, l_before, a_pack, b_pack = held
        f = m.gf[k]
        l = m.gl[k]
        a = jnp.where(k == 0, (is_first - 1.0) * 0.5 * own_inv, 0.5 * (f - f_before))
        b = jnp.where(k == 0, is_first * -0.5 * l, -0.5 * (l - l_before))
        m.aa[k] = a
        m.bb[k] = b
        return f, l, packed(k, a, a_pack), packed(k, b, b_pack)

    unused_f, unused_l, a_pack, b_pack = lax.fori_loop(0, L, slopes, (zero,) * 4, unroll=8)
    m.ysa[0] = a_pack
    m.ysa[1] = b_pack
    for side in range(2):
        for r in range(2):
            m.xsa[side, pl.ds(r * L, L), :] = m.aa[:, side_row(side, r), :]
            m.xsa[side, pl.ds((2 + r) * L, L), :] = m.bb[:, side_row(side, r), :]
    static += start([
        remote(m.xsa.at[0], m.xra.at[1], x_dev[0]),
        remote(m.xsa.at[1], m.xra.at[0], x_dev[1]),
        remote(m.ysa, m.yra.at[1], y_dev[0]),
        remote(m.ysa, m.yra.at[0], y_dev[1]),
    ])

    def predict(step, k, _):
        here = ps[k, inner, :]
        force = 0.0625 * (
            ps[k, pl.ds(PAD + 2, I), :] + ps[k, pl.ds(PAD - 2, I), :]
            + pltpu.roll(here, J - 2, 1) + pltpu.roll(here, 2, 1) - 4.0 * here)
        if step == 0:
            v = vs[k]
            force = force - 0.25 * (
                us[k, pl.ds(PAD + 1, I), :] - us[k, pl.ds(PAD - 1, I), :]
                + pltpu.roll(v, J - 1, 1) - pltpu.roll(v, 1, 1))
        else:
            force = force + m.fs[k]
        m.fs[k] = force
        m.pp[k + 1] = here + force
        return 0

    lax.fori_loop(0, L, functools.partial(predict, 0), 0, unroll=16)
    loads[6].wait()

    up_inv = zero
    messages = first
    for step in range(SUBSTEPS):
        last = step == SUBSTEPS - 1
        arrive(messages)
        rows = []
        if step == 0:
            for side in range(2):
                rows += [m.xr0[side, pl.ds(r * L, L), :] for r in range(2)]
            diff = jnp.where(sub < 2, m.yr0[0, 0], m.yr0[1, 0]) - pack
            drift = jnp.where(sub < 2, m.yr0[0, 1], m.yr0[1, 1]) - pack_v
            spin = jnp.where(sub == 1, pltpu.roll(drift, J - 1, 1),
                             jnp.where(sub == 2, -pltpu.roll(drift, 1, 1), 0.0))
            up_inv = 1.0 / m.cup[...]
        else:
            for side in range(2):
                jumps = [x_rows(step, side, h, 0) - x_rows(step, side, h - 1, 1) for h in (1, 2, 3)]
                lower = sum(m.nx[side, n, 0:2, :] * jumps[n] for n in range(3))
                upper = sum(m.nx[side, 3 + n, 0:2, :] * jumps[n] for n in range(3))
                floor = lower + 0.5 * x_rows(step, side, g_below, 2)
                for r in range(2):
                    low_r = jnp.where(level == 0, floor[r:r + 1], lower[r:r + 1])
                    rows.append(
                        m.xr[step - 1, side, pl.ds(r * L, L), :]
                        + m.xra[side, pl.ds(r * L, L), :] * low_r
                        + m.xra[side, pl.ds((2 + r) * L, L), :] * upper[r:r + 1])
            tiles = [y_tile(step, h) for h in range(groups)]
            jumps = [tiles[h] - turn8(tiles[h - 1], 1) for h in (1, 2, 3)]
            lower = sum(m.ny[n] * jumps[n] for n in range(3))
            upper = sum(m.ny[3 + n] * jumps[n] for n in range(3))
            floor = jnp.where(live8, lower + 0.5 * turn8(y_tile(step, g_below), 2), 0.0)
            wide = jnp.dot(jnp.concatenate([lower, upper, floor], 0), m.sel[...],
                           preferred_element_type=jnp.float32, precision=lax.Precision.HIGHEST)
            parts = [jnp.concatenate([wide[8 * n:8 * n + 8, J * v:J * v + J] for v in range(4)], 0)
                     for n in range(3)]
            diff = (jnp.where(sub < 2, m.yr[step - 1, 0], m.yr[step - 1, 1])
                    + m.am2[...] * jnp.where(quad == 0, parts[2], parts[0])
                    + m.bm2[...] * parts[1]) - pack
        mend2 = 0.0625 * jnp.where(sub < 2, pltpu.roll(diff, J - 2, 1), pltpu.roll(diff, 2, 1))
        mend1 = jnp.where(sub == 1, pltpu.roll(diff, J - 1, 1),
                          jnp.where(sub == 2, -pltpu.roll(diff, 1, 1), 0.0))
        adds = [0.0625 * row for row in rows]
        if step == 0:
            mend2 = mend2 - 0.25 * spin
            adds[0] = adds[0] + 0.25 * m.xr0[0, pl.ds(2 * L, L), :]
            adds[3] = adds[3] - 0.25 * m.xr0[1, pl.ds(2 * L, L), :]
        for at, add in zip((0, 1, I - 2, I - 1), adds):
            m.fs[:, at, :] = m.fs[:, at, :] + add
            m.pp[pl.ds(1, L), at, :] = m.pp[pl.ds(1, L), at, :] + add
        m.hx[0] = rows[1]
        m.hx[1] = rows[2]

        def patch(k, _):
            fix = jnp.where(edge, pltpu.roll(mend2, J - 2 - 4 * k, 1), 0.0)
            m.fs[k] = m.fs[k] + fix
            m.pp[k + 1] = m.pp[k + 1] + fix
            return 0

        lax.fori_loop(0, L, patch, 0, unroll=16)

        low = m.pp[1]
        top = m.pp[L]
        m.pp[0] = (is_first - 1.0) * low
        m.pp[L + 1] = above_sign * top
        m.pls[step] = top
        row_up = start([remote(m.pls.at[step], m.plr.at[step], peers[0])])

        def forward(k, z):
            z = (ws[k] - 0.5 * (m.pp[k + 2] - m.pp[k])) * m.im[k] + m.am[k] * z
            m.zz[k] = z
            return z

        lax.fori_loop(0, L, forward, zero, unroll=8)

        def backward(n, y):
            k = L - 1 - n
            y = m.zz[k] + m.gm[k] * y
            m.zz[k] = y
            return y

        y_low = lax.fori_loop(0, L, backward, zero, unroll=8)
        down = y_low - 0.5 * low * own_inv
        up = m.zz[L - 1] + 0.5 * top * up_inv
        m.lev[step, g, 0] = down
        m.lev[step, g, 1] = up
        group_rows = start([remote(m.lev.at[step, g], m.lev.at[step, g], dev) for dev in peers])
        if not last:
            messages = strips(step + 1, (down, up, top))

        def plain(k, held):
            before, acc = held
            y = m.zz[k]
            q = m.pp[k + 1] - 0.5 * (y - before)
            m.qs[k] = q
            return y, acc if last else packed(k, q, acc)

        ghost = y_low - (is_first * y_low - m.aa[0] * low)
        unused_y, q_pack = lax.fori_loop(0, L, plain, (ghost, zero), unroll=16)
        if not last:
            for side in range(2):
                for r in range(2):
                    m.xs[step, side, pl.ds(r * L, L), :] = m.qs[:, side_row(side, r), :]
            m.ys[step] = q_pack
            messages += start([
                remote(m.xs.at[step, 0], m.xr.at[step, 1], x_dev[0]),
                remote(m.xs.at[step, 1], m.xr.at[step, 0], x_dev[1]),
                remote(m.ys.at[step], m.yr.at[step, 1], y_dev[0]),
                remote(m.ys.at[step], m.yr.at[step, 0], y_dev[1]),
            ])


        def move(k, _):
            here = ps[k, inner, :]
            fix = jnp.where(edge, pltpu.roll(mend1, J - 2 - 4 * k, 1), 0.0)
            new_u = us[k, inner, :] - 0.25 * (
                ps[k, pl.ds(PAD + 1, I), :] - ps[k, pl.ds(PAD - 1, I), :])
            new_v = vs[k] - 0.25 * (
                pltpu.roll(here, J - 1, 1) - pltpu.roll(here, 1, 1) + fix)
            if last:
                out_u[k] = new_u
                out_v[k] = new_v
            else:
                us[k, inner, :] = new_u
                vs[k] = new_v
            return 0

        lax.fori_loop(0, L, move, 0, unroll=8)
        for end, at in ((0, 0), (1, I - 1)):
            kick = (0.25 - 0.5 * end) * m.hx[end]
            if last:
                out_u[:, at, :] = out_u[:, at, :] + kick
            else:
                us[:, PAD + at, :] = us[:, PAD + at, :] + kick

        if step == 0:
            arrive(static)
            sta = m.sta
            rows_of = inverse(sta[1, 0] + sta[0, 2], sta[2, 0] + sta[1, 2], sta[3, 0] + sta[2, 2],
                              sta[1, 1], sta[2, 1])
            for slot in range(2):
                for col in range(3):
                    m.inv[slot, col] = face_row(rows_of, col, g + slot)
            for side in range(2):
                part = lambda h, n: x_rows(0, side, h, n)
                rows_of = inverse(part(1, 0) + part(0, 2), part(2, 0) + part(1, 2),
                                  part(3, 0) + part(2, 2), part(1, 1), part(2, 1))
                for slot in range(2):
                    for col in range(3):
                        m.nx[side, 3 * slot + col, 0:2, :] = face_row(rows_of, col, g + slot)
            tiles = [y_tile(0, h) for h in range(groups)]
            part = lambda h, n: jnp.where(live8, turn8(tiles[h], n), 1.0)
            rows_of = inverse(part(1, 0) + part(0, 2), part(2, 0) + part(1, 2),
                              part(3, 0) + part(2, 2), part(1, 1), part(2, 1))
            for slot in range(2):
                for col in range(3):
                    m.ny[3 * slot + col] = jnp.where(live8, face_row(rows_of, col, g + slot), 0.0)
            m.am2[...] = jnp.where(sub < 2, m.yra[0, 0], m.yra[1, 0])
            m.bm2[...] = jnp.where(sub < 2, m.yra[0, 1], m.yra[1, 1])

        arrive(group_rows + row_up)
        jumps = [m.lev[step, h, 0] - m.lev[step, h - 1, 1] for h in (1, 2, 3)]
        under = sum(m.inv[0, n] * jumps[n] for n in range(3))
        over = sum(m.inv[1, n] * jumps[n] for n in range(3))
        under0 = under + 0.5 * m.plr[step]

        def correct(k, acc):
            x = m.zz[k] - m.gf[k] * under + m.gl[k] * over
            new = m.qs[k] + m.aa[k] * jnp.where(k == 0, under0, under) + m.bb[k] * over
            if last:
                out_w[k] = x
                out_p[k] = new
                return acc
            ws[k] = x
            ps[k, inner, :] = new
            return packed(k, new, acc)

        pack = lax.fori_loop(0, L, correct, zero, unroll=16)
        if not last:
            lax.fori_loop(0, L, functools.partial(predict, step + 1), 0, unroll=16)

    for copy in sent:
        copy.wait_send()


def store_kernel(*refs):
    sem = refs[-1]
    copies = [
        pltpu.make_async_copy(refs[n], refs[4 + n], sem.at[n]) for n in range(4)
    ]
    for copy in copies:
        copy.start()
    for copy in copies:
        copy.wait()


def body(zonal, meridional, vertical, pressure, coupling, surface, lid_flag):
    L, I, J = zonal.shape
    IP = I + 2 * PAD
    S = SUBSTEPS
    G = GROUPS
    f32 = jnp.float32
    n_sem = 5 + (G - 1) + 4 * G + 4 + S * G + (S - 1) * (4 * G + 4)
    V = lambda *shape: pltpu.VMEM(shape, f32)
    level = (L, I, J)
    scratch = dict(
        us=V(L, IP, J), vs=V(*level), ws=V(*level), ps=V(L, IP, J), cs=V(L + 1, I, J),
        ks=pltpu.VMEM((I, J), jnp.int32), ls=pltpu.VMEM((I, J), jnp.int32),
        fs=V(*level), pp=V(L + 2, I, J), zz=V(*level), qs=V(*level),
        am=V(*level), im=V(*level), gm=V(*level), gf=V(*level), gl=V(*level),
        aa=V(*level), bb=V(*level),
        xs0=V(2, 3 * L, J), ys0=V(2, I, J), xr0=V(2, 3 * L, J), yr0=V(2, 2, I, J),
        xs=V(S - 1, 2, 2 * L, J), ys=V(S - 1, I, J),
        xr=V(S - 1, 2, 2 * L, J), yr=V(S - 1, 2, I, J),
        xsa=V(2, 4 * L, J), ysa=V(2, I, J), xra=V(2, 4 * L, J), yra=V(2, 2, I, J),
        xsi=V(S, 2, 8, J), ysi=V(S, 8, J), xri=V(S, 2, G, 8, J), yri=V(S, 2, G, 8, J),
        sta=V(G, 3, I, J), lev=V(S, G, 2, I, J), cup=V(I, J),
        pls=V(S, I, J), plr=V(S, I, J), hx=V(2, L, J),
        inv=V(2, 3, I, J), nx=V(2, 6, 8, J), ny=V(6, 8, J), am2=V(I, J), bm2=V(I, J),
        sel=V(J, 4 * J),
        load_sem=pltpu.SemaphoreType.DMA((7,)),
        send_sem=pltpu.SemaphoreType.DMA((n_sem,)),
        recv_sem=pltpu.SemaphoreType.DMA((n_sem,)),
    )
    any_spec = pl.BlockSpec(memory_space=pl.ANY)
    vmem_spec = pl.BlockSpec(memory_space=pltpu.VMEM)
    field = jax.ShapeDtypeStruct(level, f32)
    results = pl.pallas_call(
        functools.partial(kernel, tuple(scratch)),
        out_shape=(V(*level),) * 4,
        in_specs=[any_spec] * 7,
        out_specs=(vmem_spec,) * 4,
        scratch_shapes=list(scratch.values()),
        compiler_params=pltpu.CompilerParams(collective_id=0, has_side_effects=True),
    )(zonal, meridional, vertical, pressure, coupling, surface, lid_flag)
    return tuple(pl.pallas_call(
        store_kernel,
        out_shape=(field,) * 4,
        in_specs=[vmem_spec] * 4,
        out_specs=(any_spec,) * 4,
        scratch_shapes=[pltpu.SemaphoreType.DMA((4,))],
        compiler_params=pltpu.CompilerParams(vmem_limit_bytes=1 << 22),
    )(*results))


def solution(mesh):
    field = P("lev", "gx", "gy")
    plane = P("gx", "gy")
    return jax.shard_map(
        body, mesh=mesh,
        in_specs=(field,) * 5 + (plane,) * 2,
        out_specs=(field,) * 4,
        check_vma=False,
    )
```

time: 44.2 us -> 38 us (0.86)
  Pallas kernels: 43.4 us -> 37.1 us
    pallas_call x1, Pallas kernels: 42.1 us -> 35.7 us  [body(): pl.pallas_call(functools.partial(kernel, tuple(scratch)), out_shape=(V(*l...]
where the time goes in v2:
time: 38 us; the launch traced here: 37.7 us
  Pallas kernels  37.1 us (98%)
  between operations  0.64 us (2%)
    pallas_call x1, Pallas kernels, body(): pl.pallas_call(functools.partial(kernel, tuple(scratch)), out_shape=(V(*l...  35.7 us
    pallas_call x1, Pallas kernels, body(): pl.pallas_call(store_kernel, out_shape=(field,) * 4, in_specs=[vmem_spec]...  1.35 us

profile of v2, /device:TPU:1, one launch (start us, length us, event | category | flops | bytes accessed | tf_op | source)
XLA Modules:
  0.0 37.7 jit_solution(11300249222175908561)
XLA Ops:
  0.6 35.7 %shard_map.102 = (f32[32,32,128]{2,1,0:T(8,128)S(1)}, f32[32,32,128]{2,1,0:T(8,128)S(1)}, f32[32,32,128]{2,1,0:T(8,128)S(1)}, f32[32,32,128]{2,1,0:T(8,128)S(1)}) custom-call(f32[32,32,128]{2,1,0:T(8,128)} %zon.1, f32[32,32,128]{2,1,0:T(8,128)} %mer.1, f32[32,32,128]{2,1,0:T(8,128)} %ver.1, f32[32,32,128]{2,1,0:T(8,128)} %pre.1, f32[32,32,128]{2,1,0:T(8,128)} %cou.1, ...), custom_call_target="tpu_custom_call" | custom-call | tf_op jit(solution)/shard_map/pallas_call | solution.py:486
  36.4 1.3 %shard_map.103 = (f32[32,32,128]{2,1,0:T(8,128)}, f32[32,32,128]{2,1,0:T(8,128)}, f32[32,32,128]{2,1,0:T(8,128)}, f32[32,32,128]{2,1,0:T(8,128)}) custom-call(f32[32,32,128]{2,1,0:T(8,128)S(1)} %get-tuple-element.8.refs_0_, f32[32,32,128]{2,1,0:T(8,128)S(1)} %get-tuple-element.9.refs_1_, f32[32,32,128]{2,1,0:T(8,128)S(1)} %get-tuple-element.10.refs_2_, ...), custom_call_target="tpu_custom_call" | custom-call | tf_op jit(solution)/shard_map/pallas_call | solution.py:494

commit v3 on v2

--- a/solution.py
+++ b/solution.py
@@ -12,6 +12,10 @@
 MESH = pl.DeviceIdType.MESH
 PAD = 8
 GROUPS = 4
+EDGES = FIRST = 0
+ROWS = EDGES + SUBSTEPS
+EXTRA = ROWS + SUBSTEPS
+STATIC = EXTRA + SUBSTEPS - 1
 
 
 def inverse(d1, d2, d3, q1, q2):
@@ -61,12 +65,13 @@
             (ver, ws),
         ])
     ]
-    for copy in loads:
-        copy.start()
     barrier = pltpu.get_barrier_semaphore()
-    everyone = peers + around
-    for dev in everyone:
+    everyone = around[:4] + peers + around[4:]
+    for n, dev in enumerate(everyone):
         pl.semaphore_signal(barrier, inc=1, device_id=dev, device_id_type=MESH)
+        if n == 6:
+            for copy in loads:
+                copy.start()
 
     lane = lax.broadcasted_iota(jnp.int32, (I, J), 1)
     level = lax.broadcasted_iota(jnp.int32, (L, J), 0)
@@ -75,37 +80,34 @@
     edge = (lane < 2) | (lane >= J - 2)
     lane8 = lax.broadcasted_iota(jnp.int32, (8, J), 1)
     quad8 = lane8 // 4
-    left8 = lane8 % 4 < 2
+    lane4 = lax.broadcasted_iota(jnp.int32, (4, J), 1)
     live8 = (quad8 % 4 == 0) & (quad8 < 16)
     zero = jnp.zeros((I, J), jnp.float32)
-    halo_rows = jnp.zeros((L, PAD, J), jnp.float32)
-    for ref in (ps, us):
-        ref[:, 0:PAD, :] = halo_rows
-        ref[:, PAD + I:, :] = halo_rows
-    pick = lax.broadcasted_iota(jnp.int32, (J, 4 * J), 0)
-    into = lax.broadcasted_iota(jnp.int32, (J, 4 * J), 1)
-    m.sel[...] = jnp.where(
-        (pick % 16 == into % 4) & (pick // 16 == into // J), 1.0, 0.0).astype(jnp.float32)
-
-    counter = iter(range(1 << 10))
-
-    def remote(src, dst, dev):
-        n = next(counter)
+    def remote(src, dst, dev, slot, send=0):
         return pltpu.make_async_remote_copy(
-            src_ref=src, dst_ref=dst, send_sem=m.send_sem.at[n], recv_sem=m.recv_sem.at[n],
+            src_ref=src, dst_ref=dst, send_sem=m.send_sem.at[send], recv_sem=m.recv_sem.at[slot],
             device_id=dev, device_id_type=MESH)
 
-    sent = []
-
-    def start(copies):
-        for copy in copies:
-            copy.start()
-        sent.extend(copies)
-        return copies
-
-    def arrive(copies):
-        for copy in copies:
-            copy.wait_recv()
+    middle = (g == 1) | (g == 2)
+    rows_sent = []
+
+    def count(ref):
+        rows = 1
+        for size in ref.shape[:-1]:
+            rows *= size
+        return rows
+
+    def start(slot, copies):
+        rows = 0
+        for src, dst, dev in copies:
+            remote(src, dst, dev, slot).start()
+            rows += count(src)
+        rows_sent.append(rows)
+        return rows
+
+    def arrive(sem, rows):
+        block = m.tally.at[pl.ds(0, rows)]
+        pltpu.make_async_copy(block, block, sem).wait()
 
     def side_row(side, r):
         return r if side == 0 else I - 2 + r
@@ -113,7 +115,7 @@
     def packed(k, plane, held):
         return jnp.where(quad == k, pltpu.roll(plane, 4 * k + 2, 1), held)
 
-    def strips(phase, planes):
+    def strips(phase, slot, planes):
         tile = jnp.zeros((8, J), jnp.float32)
         for n, plane in enumerate(planes):
             m.xsi[phase, 0, pl.ds(2 * n, 2), :] = plane[0:2]
@@ -121,13 +123,13 @@
             for v in range(4):
                 turned = pltpu.roll(plane[8 * v:8 * v + 8], 16 * v + 4 * n + 2, 1)
                 tile = jnp.where(quad8 == 4 * v + n, turned, tile)
-        m.ysi[phase] = tile
-        return start([
+        m.ysi[phase] = jnp.where(lane4 < 64, tile[0:4], pltpu.roll(tile[4:8], 64, 1))
+        return start(slot, [
             copy
             for d in range(groups) for side in range(2)
             for copy in (
-                remote(m.xsi.at[phase, side], m.xri.at[phase, 1 - side, g], around[4 * d + side]),
-                remote(m.ysi.at[phase], m.yri.at[phase, 1 - side, g], around[4 * d + 2 + side]),
+                (m.xsi.at[phase, side], m.xri.at[phase, 1 - side, g], around[4 * d + side]),
+                (m.ysi.at[phase], m.yri.at[phase, 1 - side, g], around[4 * d + 2 + side]),
             )
         ])
 
@@ -135,36 +137,42 @@
         return m.xri[phase, side, h, pl.ds(2 * n, 2), :]
 
     def y_tile(phase, h):
-        return jnp.where(left8, m.yri[phase, 0, h], m.yri[phase, 1, h])
+        half = jnp.where(lane4 % 4 < 2, m.yri[phase, 0, h], m.yri[phase, 1, h])
+        return jnp.concatenate([half, pltpu.roll(half, 64, 1)], 0)
 
     def turn8(tile, n):
         return pltpu.roll(tile, J - 4 * n, 1) if n else tile
 
+    for step in range(SUBSTEPS - 1):
+        m.lex[step] = zero
     loads[0].wait()
-    loads[1].wait()
-    loads[2].wait()
     for side in range(2):
         for r in range(2):
             m.xs0[side, pl.ds(r * L, L), :] = ps[:, PAD + side_row(side, r), :]
+    pack = lax.fori_loop(0, L, lambda k, acc: packed(k, ps[k, inner, :], acc), zero, unroll=16)
+    m.ys0[0] = pack
+    loads[1].wait()
+    pack_v = lax.fori_loop(0, L, lambda k, acc: packed(k, vs[k], acc), zero, unroll=16)
+    m.ys0[1] = pack_v
+    loads[2].wait()
+    for side in range(2):
         m.xs0[side, pl.ds(2 * L, L), :] = us[:, PAD + (I - 1) * side, :]
-
-    def pack0(k, held):
-        return packed(k, ps[k, inner, :], held[0]), packed(k, vs[k], held[1])
-
-    pack, pack_v = lax.fori_loop(0, L, pack0, (zero, zero), unroll=16)
-    m.ys0[0] = pack
-    m.ys0[1] = pack_v
     for n in range(3, 6):
         loads[n].wait()
 
     pl.semaphore_wait(barrier, len(everyone))
-    first = start([
-        remote(m.xs0.at[0], m.xr0.at[1], x_dev[0]),
-        remote(m.xs0.at[1], m.xr0.at[0], x_dev[1]),
-        remote(m.ys0, m.yr0.at[1], y_dev[0]),
-        remote(m.ys0, m.yr0.at[0], y_dev[1]),
-        remote(cs.at[0], m.cup, peers[-1]),
+    messages = start(FIRST, [
+        (m.xs0.at[0], m.xr0.at[1], x_dev[0]),
+        (m.xs0.at[1], m.xr0.at[0], x_dev[1]),
+        (m.ys0, m.yr0.at[1], y_dev[0]),
+        (m.ys0, m.yr0.at[0], y_dev[1]),
+        (cs.at[0], m.cup, peers[-1]),
     ])
+
+    halo_rows = jnp.zeros((L, PAD, J), jnp.float32)
+    for ref in (ps, us):
+        ref[:, 0:PAD, :] = halo_rows
+        ref[:, PAD + I:, :] = halo_rows
 
     cs[L] = zero
     height = m.ks[...] - g * L
@@ -207,12 +215,8 @@
     own_static = (m.gf[0] + own_inv, m.gf[L - 1], m.gl[L - 1])
     for n in range(3):
         m.sta[g, n] = own_static[n]
-    static = start([remote(m.sta.at[g], m.sta.at[g], dev) for dev in peers])
-    spare = jnp.zeros((2, J), jnp.float32)
-    for phase in range(SUBSTEPS):
-        for side in range(2):
-            m.xsi[phase, side, pl.ds(6, 2), :] = spare
-    static += strips(0, own_static)
+    static = start(STATIC, [(m.sta.at[g], m.sta.at[g], dev) for dev in peers])
+    static += strips(0, STATIC, own_static)
 
     def slopes(k, held):
         f_before, l_before, a_pack, b_pack = held
@@ -231,12 +235,17 @@
         for r in range(2):
             m.xsa[side, pl.ds(r * L, L), :] = m.aa[:, side_row(side, r), :]
             m.xsa[side, pl.ds((2 + r) * L, L), :] = m.bb[:, side_row(side, r), :]
-    static += start([
-        remote(m.xsa.at[0], m.xra.at[1], x_dev[0]),
-        remote(m.xsa.at[1], m.xra.at[0], x_dev[1]),
-        remote(m.ysa, m.yra.at[1], y_dev[0]),
-        remote(m.ysa, m.yra.at[0], y_dev[1]),
+    static += start(STATIC, [
+        (m.xsa.at[0], m.xra.at[1], x_dev[0]),
+        (m.xsa.at[1], m.xra.at[0], x_dev[1]),
+        (m.ysa, m.yra.at[1], y_dev[0]),
+        (m.ysa, m.yra.at[0], y_dev[1]),
     ])
+
+    pick = lax.broadcasted_iota(jnp.int32, (J, 4 * J), 0)
+    into = lax.broadcasted_iota(jnp.int32, (J, 4 * J), 1)
+    m.sel[...] = jnp.where(
+        (pick % 16 == into % 4) & (pick // 16 == into // J), 1.0, 0.0).astype(jnp.bfloat16)
 
     def predict(step, k, _):
         here = ps[k, inner, :]
@@ -258,10 +267,9 @@
     loads[6].wait()
 
     up_inv = zero
-    messages = first
     for step in range(SUBSTEPS):
         last = step == SUBSTEPS - 1
-        arrive(messages)
+        arrive(m.recv_sem.at[EDGES + step], messages)
         rows = []
         if step == 0:
             for side in range(2):
@@ -288,8 +296,14 @@
             lower = sum(m.ny[n] * jumps[n] for n in range(3))
             upper = sum(m.ny[3 + n] * jumps[n] for n in range(3))
             floor = jnp.where(live8, lower + 0.5 * turn8(y_tile(step, g_below), 2), 0.0)
-            wide = jnp.dot(jnp.concatenate([lower, upper, floor], 0), m.sel[...],
-                           preferred_element_type=jnp.float32, precision=lax.Precision.HIGHEST)
+            whole = jnp.concatenate([lower, upper, floor], 0)
+            coarse = whole.astype(jnp.bfloat16)
+            rest = whole - coarse.astype(jnp.float32)
+            second = rest.astype(jnp.bfloat16)
+            fine = (rest - second.astype(jnp.float32)).astype(jnp.bfloat16)
+            wide = (jnp.dot(fine, m.sel[...], preferred_element_type=jnp.float32)
+                    + jnp.dot(second, m.sel[...], preferred_element_type=jnp.float32)
+                    + jnp.dot(coarse, m.sel[...], preferred_element_type=jnp.float32))
             parts = [jnp.concatenate([wide[8 * n:8 * n + 8, J * v:J * v + J] for v in range(4)], 0)
                      for n in range(3)]
             diff = (jnp.where(sub < 2, m.yr[step - 1, 0], m.yr[step - 1, 1])
@@ -309,27 +323,27 @@
         m.hx[0] = rows[1]
         m.hx[1] = rows[2]
 
-        def patch(k, _):
+        def eliminate(k, z, mid_above, mid_below):
+            z = (ws[k] - 0.5 * (mid_above - mid_below)) * m.im[k] + m.am[k] * z
+            m.zz[k] = z
+            return z
+
+        def forward(k, held):
+            z, one_below, two_below = held
             fix = jnp.where(edge, pltpu.roll(mend2, J - 2 - 4 * k, 1), 0.0)
             m.fs[k] = m.fs[k] + fix
-            m.pp[k + 1] = m.pp[k + 1] + fix
-            return 0
-
-        lax.fori_loop(0, L, patch, 0, unroll=16)
-
+            here = m.pp[k + 1] + fix
+            m.pp[k + 1] = here
+            z = eliminate(jnp.maximum(k - 1, 0), z, here, two_below)
+            z = jnp.where(k == 0, 0.0, z)
+            one_below = jnp.where(k == 0, (is_first - 1.0) * here, one_below)
+            return z, here, one_below
+
+        z, top, under_top = lax.fori_loop(0, L, forward, (zero,) * 3, unroll=16)
+        m.pls[step] = top
+        group_rows = start(ROWS + step, [(m.pls.at[step], m.plr.at[step], peers[0])])
+        eliminate(L - 1, z, above_sign * top, under_top)
         low = m.pp[1]
-        top = m.pp[L]
-        m.pp[0] = (is_first - 1.0) * low
-        m.pp[L + 1] = above_sign * top
-        m.pls[step] = top
-        row_up = start([remote(m.pls.at[step], m.plr.at[step], peers[0])])
-
-        def forward(k, z):
-            z = (ws[k] - 0.5 * (m.pp[k + 2] - m.pp[k])) * m.im[k] + m.am[k] * z
-            m.zz[k] = z
-            return z
-
-        lax.fori_loop(0, L, forward, zero, unroll=8)
 
         def backward(n, y):
             k = L - 1 - n
@@ -340,11 +354,22 @@
         y_low = lax.fori_loop(0, L, backward, zero, unroll=8)
         down = y_low - 0.5 * low * own_inv
         up = m.zz[L - 1] + 0.5 * top * up_inv
-        m.lev[step, g, 0] = down
-        m.lev[step, g, 1] = up
-        group_rows = start([remote(m.lev.at[step, g], m.lev.at[step, g], dev) for dev in peers])
-        if not last:
-            messages = strips(step + 1, (down, up, top))
+        if step == 0:
+            m.lev[g, 0] = down
+            m.lev[g, 1] = up
+            group_rows += start(ROWS, [(m.lev.at[g], m.lev.at[g], dev) for dev in peers])
+            messages = strips(1, EDGES + 1, (down, up, top))
+        else:
+            if not last:
+                messages = strips(step + 1, EDGES + step + 1, (down, up, top))
+            for d in range(3):
+                m.lvs[step - 1, d] = m.mix[0, d] * down + m.mix[1, d] * up
+            group_rows += start(ROWS + step, [
+                (m.lvs.at[step - 1, d], m.lvr.at[step - 1, d], peers[d]) for d in range(3)])
+            m.les[step - 1] = up
+            extra = remote(m.les.at[step - 1], m.lex.at[step - 1], {"lev": groups - 1 - g},
+                           EXTRA + step - 1, step)
+            pl.when(middle)(extra.start)
 
         def plain(k, held):
             before, acc = held
@@ -360,11 +385,11 @@
                 for r in range(2):
                     m.xs[step, side, pl.ds(r * L, L), :] = m.qs[:, side_row(side, r), :]
             m.ys[step] = q_pack
-            messages += start([
-                remote(m.xs.at[step, 0], m.xr.at[step, 1], x_dev[0]),
-                remote(m.xs.at[step, 1], m.xr.at[step, 0], x_dev[1]),
-                remote(m.ys.at[step], m.yr.at[step, 1], y_dev[0]),
-                remote(m.ys.at[step], m.yr.at[step, 0], y_dev[1]),
+            messages += start(EDGES + step + 1, [
+                (m.xs.at[step, 0], m.xr.at[step, 1], x_dev[0]),
+                (m.xs.at[step, 1], m.xr.at[step, 0], x_dev[1]),
+                (m.ys.at[step], m.yr.at[step, 1], y_dev[0]),
+                (m.ys.at[step], m.yr.at[step, 0], y_dev[1]),
             ])
 
 
@@ -392,13 +417,35 @@
                 us[:, PAD + at, :] = us[:, PAD + at, :] + kick
 
         if step == 0:
-            arrive(static)
+            arrive(m.recv_sem.at[STATIC], static)
             sta = m.sta
             rows_of = inverse(sta[1, 0] + sta[0, 2], sta[2, 0] + sta[1, 2], sta[3, 0] + sta[2, 2],
                               sta[1, 1], sta[2, 1])
             for slot in range(2):
+                face = g + slot
+                row = [face_row(rows_of, col, face) for col in range(3)]
                 for col in range(3):
-                    m.inv[slot, col] = face_row(rows_of, col, g + slot)
+                    m.inv[slot, col] = row[col]
+                mine = jnp.where((face >= 1) & (face <= 3), 1.0, 0.0).astype(jnp.float32)
+
+                def of(h):
+                    return jnp.where(h == 1, row[0], jnp.where(h == 2, row[1], row[2]))
+
+                for d in range(3):
+                    o = lax.rem(g + groups - 1 - d, groups)
+                    m.cw[slot, d] = jnp.where(o == 0, -row[0], jnp.where(
+                        o == groups - 1, row[2], jnp.where(middle, of(o), mine)))
+                m.cw[slot, 3] = jnp.where(g == 0, 0.0, of(g))
+                m.cw[slot, 4] = jnp.where(g == groups - 1, 0.0, -of(g + 1))
+                m.cw[slot, 5] = jnp.where(middle, -of(groups - g), 0.0)
+            for d in range(3):
+                to = lax.rem(g + 1 + d, groups)
+                row = [jnp.where(to == 0, rows_of[0][col], rows_of[2][col]) for col in range(3)]
+                raw = (to == 1) | (to == 2)
+                m.mix[0, d] = jnp.where(g == 0, 0.0, jnp.where((g == groups - 1) | raw, 1.0, jnp.where(
+                    g == 1, row[0], row[1])))
+                m.mix[1, d] = jnp.where(g == 0, 1.0, jnp.where((g == groups - 1) | raw, 0.0, jnp.where(
+                    g == 1, -row[1], -row[2])))
             for side in range(2):
                 part = lambda h, n: x_rows(0, side, h, n)
                 rows_of = inverse(part(1, 0) + part(0, 2), part(2, 0) + part(1, 2),
@@ -416,10 +463,16 @@
             m.am2[...] = jnp.where(sub < 2, m.yra[0, 0], m.yra[1, 0])
             m.bm2[...] = jnp.where(sub < 2, m.yra[0, 1], m.yra[1, 1])
 
-        arrive(group_rows + row_up)
-        jumps = [m.lev[step, h, 0] - m.lev[step, h - 1, 1] for h in (1, 2, 3)]
-        under = sum(m.inv[0, n] * jumps[n] for n in range(3))
-        over = sum(m.inv[1, n] * jumps[n] for n in range(3))
+        arrive(m.recv_sem.at[ROWS + step], group_rows)
+        if step == 0:
+            jumps = [m.lev[h, 0] - m.lev[h - 1, 1] for h in (1, 2, 3)]
+            under = sum(m.inv[0, n] * jumps[n] for n in range(3))
+            over = sum(m.inv[1, n] * jumps[n] for n in range(3))
+        else:
+            pl.when(middle)(extra.wait)
+            terms = [m.lvr[step - 1, d] for d in range(3)] + [down, up, m.lex[step - 1]]
+            under = sum(m.cw[0, n] * terms[n] for n in range(6))
+            over = sum(m.cw[1, n] * terms[n] for n in range(6))
         under0 = under + 0.5 * m.plr[step]
 
         def correct(k, acc):
@@ -437,8 +490,7 @@
         if not last:
             lax.fori_loop(0, L, functools.partial(predict, step + 1), 0, unroll=16)
 
-    for copy in sent:
-        copy.wait_send()
+    arrive(m.send_sem.at[0], sum(rows_sent))
 
 
 def store_kernel(*refs):
@@ -458,7 +510,6 @@
     S = SUBSTEPS
     G = GROUPS
     f32 = jnp.float32
-    n_sem = 5 + (G - 1) + 4 * G + 4 + S * G + (S - 1) * (4 * G + 4)
     V = lambda *shape: pltpu.VMEM(shape, f32)
     level = (L, I, J)
     scratch = dict(
@@ -471,14 +522,16 @@
         xs=V(S - 1, 2, 2 * L, J), ys=V(S - 1, I, J),
         xr=V(S - 1, 2, 2 * L, J), yr=V(S - 1, 2, I, J),
         xsa=V(2, 4 * L, J), ysa=V(2, I, J), xra=V(2, 4 * L, J), yra=V(2, 2, I, J),
-        xsi=V(S, 2, 8, J), ysi=V(S, 8, J), xri=V(S, 2, G, 8, J), yri=V(S, 2, G, 8, J),
-        sta=V(G, 3, I, J), lev=V(S, G, 2, I, J), cup=V(I, J),
-        pls=V(S, I, J), plr=V(S, I, J), hx=V(2, L, J),
+        xsi=V(S, 2, 6, J), ysi=V(S, 4, J), xri=V(S, 2, G, 6, J), yri=V(S, 2, G, 4, J),
+        sta=V(G, 3, I, J), lev=V(G, 2, I, J), cup=V(I, J),
+        lvs=V(S - 1, 3, I, J), lvr=V(S - 1, 3, I, J), les=V(S - 1, I, J), lex=V(S - 1, I, J),
+        mix=V(2, 3, I, J), cw=V(2, 6, I, J), pls=V(S, I, J), plr=V(S, I, J), hx=V(2, L, J),
         inv=V(2, 3, I, J), nx=V(2, 6, 8, J), ny=V(6, 8, J), am2=V(I, J), bm2=V(I, J),
-        sel=V(J, 4 * J),
+        sel=pltpu.VMEM((J, 4 * J), jnp.bfloat16),
         load_sem=pltpu.SemaphoreType.DMA((7,)),
-        send_sem=pltpu.SemaphoreType.DMA((n_sem,)),
-        recv_sem=pltpu.SemaphoreType.DMA((n_sem,)),
+        tally=V(2560, J),
+        send_sem=pltpu.SemaphoreType.DMA((S,)),
+        recv_sem=pltpu.SemaphoreType.DMA((STATIC + 1,)),
     )
     any_spec = pl.BlockSpec(memory_space=pl.ANY)
     vmem_spec = pl.BlockSpec(memory_space=pltpu.VMEM)

time: 38 us -> 35.8 us (0.942)
  Pallas kernels: 37.1 us -> 35.1 us
    pallas_call x1, Pallas kernels: 35.7 us -> 33.7 us  [body(): pl.pallas_call(functools.partial(kernel, tuple(scratch)), out_shape=(V(*l...]
where the time goes in v3:
time: 35.8 us; the launch traced here: 35.7 us
  Pallas kernels  35.1 us (98%)
  between operations  0.64 us (2%)
    pallas_call x1, Pallas kernels, body(): pl.pallas_call(functools.partial(kernel, tuple(scratch)), out_shape=(V(*l...  33.7 us
    pallas_call x1, Pallas kernels, body(): pl.pallas_call(store_kernel, out_shape=(field,) * 4, in_specs=[vmem_spec]...  1.35 us

profile of v3, /device:TPU:1, one launch (start us, length us, event | category | flops | bytes accessed | tf_op | source)
XLA Modules:
  0.0 35.7 jit_solution(1178420681709028434)
XLA Ops:
  0.6 33.7 %shard_map.102 = (f32[32,32,128]{2,1,0:T(8,128)S(1)}, f32[32,32,128]{2,1,0:T(8,128)S(1)}, f32[32,32,128]{2,1,0:T(8,128)S(1)}, f32[32,32,128]{2,1,0:T(8,128)S(1)}) custom-call(f32[32,32,128]{2,1,0:T(8,128)} %zon.1, f32[32,32,128]{2,1,0:T(8,128)} %mer.1, f32[32,32,128]{2,1,0:T(8,128)} %ver.1, f32[32,32,128]{2,1,0:T(8,128)} %pre.1, f32[32,32,128]{2,1,0:T(8,128)} %cou.1, ...), custom_call_target="tpu_custom_call" | custom-call | tf_op jit(solution)/shard_map/pallas_call | solution.py:539
  34.4 1.3 %shard_map.103 = (f32[32,32,128]{2,1,0:T(8,128)}, f32[32,32,128]{2,1,0:T(8,128)}, f32[32,32,128]{2,1,0:T(8,128)}, f32[32,32,128]{2,1,0:T(8,128)}) custom-call(f32[32,32,128]{2,1,0:T(8,128)S(1)} %get-tuple-element.8.refs_0_, f32[32,32,128]{2,1,0:T(8,128)S(1)} %get-tuple-element.9.refs_1_, f32[32,32,128]{2,1,0:T(8,128)S(1)} %get-tuple-element.10.refs_2_, ...), custom_call_target="tpu_custom_call" | custom-call | tf_op jit(solution)/shard_map/pallas_call | solution.py:547

commit v4 on v3

--- a/solution.py
+++ b/solution.py
@@ -66,12 +66,11 @@
         ])
     ]
     barrier = pltpu.get_barrier_semaphore()
-    everyone = around[:4] + peers + around[4:]
-    for n, dev in enumerate(everyone):
+    near = around[:4] + peers
+    for dev in near:
         pl.semaphore_signal(barrier, inc=1, device_id=dev, device_id_type=MESH)
-        if n == 6:
-            for copy in loads:
-                copy.start()
+    for copy in loads:
+        copy.start()
 
     lane = lax.broadcasted_iota(jnp.int32, (I, J), 1)
     level = lax.broadcasted_iota(jnp.int32, (L, J), 0)
@@ -114,6 +113,9 @@
 
     def packed(k, plane, held):
         return jnp.where(quad == k, pltpu.roll(plane, 4 * k + 2, 1), held)
+
+    def swapped(held):
+        return jnp.where(sub < 2, pltpu.roll(held, J - 2, 1), pltpu.roll(held, 2, 1))
 
     def strips(phase, slot, planes):
         tile = jnp.zeros((8, J), jnp.float32)
@@ -160,7 +162,9 @@
     for n in range(3, 6):
         loads[n].wait()
 
-    pl.semaphore_wait(barrier, len(everyone))
+    pl.semaphore_wait(barrier, len(near))
+    for dev in around[:4]:
+        pl.semaphore_signal(m.hood, inc=1, device_id=dev, device_id_type=MESH)
     messages = start(FIRST, [
         (m.xs0.at[0], m.xr0.at[1], x_dev[0]),
         (m.xs0.at[1], m.xr0.at[0], x_dev[1]),
@@ -216,7 +220,7 @@
     for n in range(3):
         m.sta[g, n] = own_static[n]
     static = start(STATIC, [(m.sta.at[g], m.sta.at[g], dev) for dev in peers])
-    static += strips(0, STATIC, own_static)
+
 
     def slopes(k, held):
         f_before, l_before, a_pack, b_pack = held
@@ -245,7 +249,7 @@
     pick = lax.broadcasted_iota(jnp.int32, (J, 4 * J), 0)
     into = lax.broadcasted_iota(jnp.int32, (J, 4 * J), 1)
     m.sel[...] = jnp.where(
-        (pick % 16 == into % 4) & (pick // 16 == into // J), 1.0, 0.0).astype(jnp.bfloat16)
+        (pick % 16 == (into + 2) % 4) & (pick // 16 == into // J), 1.0, 0.0).astype(jnp.bfloat16)
 
     def predict(step, k, _):
         here = ps[k, inner, :]
@@ -265,6 +269,8 @@
 
     lax.fori_loop(0, L, functools.partial(predict, 0), 0, unroll=16)
     loads[6].wait()
+    pl.semaphore_wait(m.hood, 4)
+    static += strips(0, STATIC, [m.sta[g, n] for n in range(3)])
 
     up_inv = zero
     for step in range(SUBSTEPS):
@@ -274,7 +280,7 @@
         if step == 0:
             for side in range(2):
                 rows += [m.xr0[side, pl.ds(r * L, L), :] for r in range(2)]
-            diff = jnp.where(sub < 2, m.yr0[0, 0], m.yr0[1, 0]) - pack
+            diff = swapped(jnp.where(sub < 2, m.yr0[0, 0], m.yr0[1, 0]) - pack)
             drift = jnp.where(sub < 2, m.yr0[0, 1], m.yr0[1, 1]) - pack_v
             spin = jnp.where(sub == 1, pltpu.roll(drift, J - 1, 1),
                              jnp.where(sub == 2, -pltpu.roll(drift, 1, 1), 0.0))
@@ -306,12 +312,12 @@
                     + jnp.dot(coarse, m.sel[...], preferred_element_type=jnp.float32))
             parts = [jnp.concatenate([wide[8 * n:8 * n + 8, J * v:J * v + J] for v in range(4)], 0)
                      for n in range(3)]
-            diff = (jnp.where(sub < 2, m.yr[step - 1, 0], m.yr[step - 1, 1])
+            diff = (swapped(jnp.where(sub < 2, m.yr[step - 1, 0], m.yr[step - 1, 1]) - pack)
                     + m.am2[...] * jnp.where(quad == 0, parts[2], parts[0])
-                    + m.bm2[...] * parts[1]) - pack
-        mend2 = 0.0625 * jnp.where(sub < 2, pltpu.roll(diff, J - 2, 1), pltpu.roll(diff, 2, 1))
-        mend1 = jnp.where(sub == 1, pltpu.roll(diff, J - 1, 1),
-                          jnp.where(sub == 2, -pltpu.roll(diff, 1, 1), 0.0))
+                    + m.bm2[...] * parts[1])
+        mend2 = 0.0625 * diff
+        mend1 = jnp.where(sub == 1, pltpu.roll(diff, 1, 1),
+                          jnp.where(sub == 2, -pltpu.roll(diff, J - 1, 1), 0.0))
         adds = [0.0625 * row for row in rows]
         if step == 0:
             mend2 = mend2 - 0.25 * spin
@@ -339,7 +345,7 @@
             one_below = jnp.where(k == 0, (is_first - 1.0) * here, one_below)
             return z, here, one_below
 
-        z, top, under_top = lax.fori_loop(0, L, forward, (zero,) * 3, unroll=16)
+        z, top, under_top = lax.fori_loop(0, L, forward, (zero,) * 3, unroll=32)
         m.pls[step] = top
         group_rows = start(ROWS + step, [(m.pls.at[step], m.plr.at[step], peers[0])])
         eliminate(L - 1, z, above_sign * top, under_top)
@@ -460,8 +466,8 @@
             for slot in range(2):
                 for col in range(3):
                     m.ny[3 * slot + col] = jnp.where(live8, face_row(rows_of, col, g + slot), 0.0)
-            m.am2[...] = jnp.where(sub < 2, m.yra[0, 0], m.yra[1, 0])
-            m.bm2[...] = jnp.where(sub < 2, m.yra[0, 1], m.yra[1, 1])
+            m.am2[...] = swapped(jnp.where(sub < 2, m.yra[0, 0], m.yra[1, 0]))
+            m.bm2[...] = swapped(jnp.where(sub < 2, m.yra[0, 1], m.yra[1, 1]))
 
         arrive(m.recv_sem.at[ROWS + step], group_rows)
         if step == 0:
@@ -486,9 +492,9 @@
             ps[k, inner, :] = new
             return packed(k, new, acc)
 
-        pack = lax.fori_loop(0, L, correct, zero, unroll=16)
+        pack = lax.fori_loop(0, L, correct, zero, unroll=32)
         if not last:
-            lax.fori_loop(0, L, functools.partial(predict, step + 1), 0, unroll=16)
+            lax.fori_loop(0, L, functools.partial(predict, step + 1), 0, unroll=32)
 
     arrive(m.send_sem.at[0], sum(rows_sent))
 
@@ -529,7 +535,7 @@
         inv=V(2, 3, I, J), nx=V(2, 6, 8, J), ny=V(6, 8, J), am2=V(I, J), bm2=V(I, J),
         sel=pltpu.VMEM((J, 4 * J), jnp.bfloat16),
         load_sem=pltpu.SemaphoreType.DMA((7,)),
-        tally=V(2560, J),
+        tally=V(2560, J), hood=pltpu.SemaphoreType.REGULAR,
         send_sem=pltpu.SemaphoreType.DMA((S,)),
         recv_sem=pltpu.SemaphoreType.DMA((STATIC + 1,)),
     )

time: 35.8 us -> 33.6 us (0.939)
  Pallas kernels: 35.1 us -> 32.8 us
    pallas_call x1, Pallas kernels: 33.7 us -> 31.5 us  [body(): pl.pallas_call(functools.partial(kernel, tuple(scratch)), out_shape=(V(*l...]
where the time goes in v4:
time: 33.6 us; the launch traced here: 33.5 us
  Pallas kernels  32.8 us (98%)
  between operations  0.64 us (2%)
    pallas_call x1, Pallas kernels, body(): pl.pallas_call(functools.partial(kernel, tuple(scratch)), out_shape=(V(*l...  31.5 us
    pallas_call x1, Pallas kernels, body(): pl.pallas_call(store_kernel, out_shape=(field,) * 4, in_specs=[vmem_spec]...  1.35 us

profile of v4, /device:TPU:1, one launch (start us, length us, event | category | flops | bytes accessed | tf_op | source)
XLA Modules:
  0.0 33.5 jit_solution(12504900552872251241)
XLA Ops:
  0.6 31.5 %shard_map.102 = (f32[32,32,128]{2,1,0:T(8,128)S(1)}, f32[32,32,128]{2,1,0:T(8,128)S(1)}, f32[32,32,128]{2,1,0:T(8,128)S(1)}, f32[32,32,128]{2,1,0:T(8,128)S(1)}) custom-call(f32[32,32,128]{2,1,0:T(8,128)} %zon.1, f32[32,32,128]{2,1,0:T(8,128)} %mer.1, f32[32,32,128]{2,1,0:T(8,128)} %ver.1, f32[32,32,128]{2,1,0:T(8,128)} %pre.1, f32[32,32,128]{2,1,0:T(8,128)} %cou.1, ...), custom_call_target="tpu_custom_call" | custom-call | tf_op jit(solution)/shard_map/pallas_call | solution.py:545
  32.1 1.3 %shard_map.103 = (f32[32,32,128]{2,1,0:T(8,128)}, f32[32,32,128]{2,1,0:T(8,128)}, f32[32,32,128]{2,1,0:T(8,128)}, f32[32,32,128]{2,1,0:T(8,128)}) custom-call(f32[32,32,128]{2,1,0:T(8,128)S(1)} %get-tuple-element.8.refs_0_, f32[32,32,128]{2,1,0:T(8,128)S(1)} %get-tuple-element.9.refs_1_, f32[32,32,128]{2,1,0:T(8,128)S(1)} %get-tuple-element.10.refs_2_, ...), custom_call_target="tpu_custom_call" | custom-call | tf_op jit(solution)/shard_map/pallas_call | solution.py:553

commit v5 on v4

--- a/solution.py
+++ b/solution.py
@@ -12,6 +12,7 @@
 MESH = pl.DeviceIdType.MESH
 PAD = 8
 GROUPS = 4
+FAR_FIRST = (1, 0, 2)
 EDGES = FIRST = 0
 ROWS = EDGES + SUBSTEPS
 EXTRA = ROWS + SUBSTEPS
@@ -128,7 +129,7 @@
         m.ysi[phase] = jnp.where(lane4 < 64, tile[0:4], pltpu.roll(tile[4:8], 64, 1))
         return start(slot, [
             copy
-            for d in range(groups) for side in range(2)
+            for d in (2, 1, 3, 0) for side in range(2)
             for copy in (
                 (m.xsi.at[phase, side], m.xri.at[phase, 1 - side, g], around[4 * d + side]),
                 (m.ysi.at[phase], m.yri.at[phase, 1 - side, g], around[4 * d + 2 + side]),
@@ -151,11 +152,12 @@
     for side in range(2):
         for r in range(2):
             m.xs0[side, pl.ds(r * L, L), :] = ps[:, PAD + side_row(side, r), :]
-    pack = lax.fori_loop(0, L, lambda k, acc: packed(k, ps[k, inner, :], acc), zero, unroll=16)
-    m.ys0[0] = pack
+    pack = lax.fori_loop(0, L, lambda k, acc: packed(k, ps[k, inner, :], acc), zero, unroll=32)
     loads[1].wait()
-    pack_v = lax.fori_loop(0, L, lambda k, acc: packed(k, vs[k], acc), zero, unroll=16)
-    m.ys0[1] = pack_v
+    pack_v = lax.fori_loop(0, L, lambda k, acc: packed(k, vs[k], acc), zero, unroll=32)
+    v_up = pltpu.roll(pack_v, 1, 1)
+    m.ys0[0] = jnp.where(sub < 2, pltpu.roll(pack, J - 2, 1), pack_v)
+    m.ys0[1] = jnp.where(sub < 2, pack, v_up)
     loads[2].wait()
     for side in range(2):
         m.xs0[side, pl.ds(2 * L, L), :] = us[:, PAD + (I - 1) * side, :]
@@ -168,8 +170,8 @@
     messages = start(FIRST, [
         (m.xs0.at[0], m.xr0.at[1], x_dev[0]),
         (m.xs0.at[1], m.xr0.at[0], x_dev[1]),
-        (m.ys0, m.yr0.at[1], y_dev[0]),
-        (m.ys0, m.yr0.at[0], y_dev[1]),
+        (m.ys0.at[0], m.yr0.at[1], y_dev[0]),
+        (m.ys0.at[1], m.yr0.at[0], y_dev[1]),
         (cs.at[0], m.cup, peers[-1]),
     ])
 
@@ -219,7 +221,7 @@
     own_static = (m.gf[0] + own_inv, m.gf[L - 1], m.gl[L - 1])
     for n in range(3):
         m.sta[g, n] = own_static[n]
-    static = start(STATIC, [(m.sta.at[g], m.sta.at[g], dev) for dev in peers])
+    static = start(STATIC, [(m.sta.at[g], m.sta.at[g], peers[d]) for d in FAR_FIRST])
 
 
     def slopes(k, held):
@@ -280,10 +282,9 @@
         if step == 0:
             for side in range(2):
                 rows += [m.xr0[side, pl.ds(r * L, L), :] for r in range(2)]
-            diff = swapped(jnp.where(sub < 2, m.yr0[0, 0], m.yr0[1, 0]) - pack)
-            drift = jnp.where(sub < 2, m.yr0[0, 1], m.yr0[1, 1]) - pack_v
-            spin = jnp.where(sub == 1, pltpu.roll(drift, J - 1, 1),
-                             jnp.where(sub == 2, -pltpu.roll(drift, 1, 1), 0.0))
+            diff = jnp.where(sub < 2, m.yr0[1], pltpu.roll(m.yr0[0], 2, 1)) - swapped(pack)
+            spin = jnp.where(sub == 1, pltpu.roll(m.yr0[1] - pack_v, J - 1, 1),
+                             jnp.where(sub == 2, v_up - m.yr0[0], 0.0))
             up_inv = 1.0 / m.cup[...]
         else:
             for side in range(2):
@@ -303,13 +304,11 @@
             upper = sum(m.ny[3 + n] * jumps[n] for n in range(3))
             floor = jnp.where(live8, lower + 0.5 * turn8(y_tile(step, g_below), 2), 0.0)
             whole = jnp.concatenate([lower, upper, floor], 0)
-            coarse = whole.astype(jnp.bfloat16)
-            rest = whole - coarse.astype(jnp.float32)
-            second = rest.astype(jnp.bfloat16)
-            fine = (rest - second.astype(jnp.float32)).astype(jnp.bfloat16)
-            wide = (jnp.dot(fine, m.sel[...], preferred_element_type=jnp.float32)
-                    + jnp.dot(second, m.sel[...], preferred_element_type=jnp.float32)
-                    + jnp.dot(coarse, m.sel[...], preferred_element_type=jnp.float32))
+            coarse = whole.astype(jnp.bfloat16).astype(jnp.float32)
+            second = (whole - coarse).astype(jnp.bfloat16).astype(jnp.float32)
+            pieces = jnp.concatenate([whole - coarse - second, second, coarse], 0)
+            wide = jnp.dot(pieces.astype(jnp.bfloat16), m.sel[...], preferred_element_type=jnp.float32)
+            wide = wide[0:24] + wide[24:48] + wide[48:72]
             parts = [jnp.concatenate([wide[8 * n:8 * n + 8, J * v:J * v + J] for v in range(4)], 0)
                      for n in range(3)]
             diff = (swapped(jnp.where(sub < 2, m.yr[step - 1, 0], m.yr[step - 1, 1]) - pack)
@@ -363,7 +362,7 @@
         if step == 0:
             m.lev[g, 0] = down
             m.lev[g, 1] = up
-            group_rows += start(ROWS, [(m.lev.at[g], m.lev.at[g], dev) for dev in peers])
+            group_rows += start(ROWS, [(m.lev.at[g], m.lev.at[g], peers[d]) for d in FAR_FIRST])
             messages = strips(1, EDGES + 1, (down, up, top))
         else:
             if not last:
@@ -371,7 +370,7 @@
             for d in range(3):
                 m.lvs[step - 1, d] = m.mix[0, d] * down + m.mix[1, d] * up
             group_rows += start(ROWS + step, [
-                (m.lvs.at[step - 1, d], m.lvr.at[step - 1, d], peers[d]) for d in range(3)])
+                (m.lvs.at[step - 1, d], m.lvr.at[step - 1, d], peers[d]) for d in FAR_FIRST])
             m.les[step - 1] = up
             extra = remote(m.les.at[step - 1], m.lex.at[step - 1], {"lev": groups - 1 - g},
                            EXTRA + step - 1, step)
@@ -385,7 +384,7 @@
             return y, acc if last else packed(k, q, acc)
 
         ghost = y_low - (is_first * y_low - m.aa[0] * low)
-        unused_y, q_pack = lax.fori_loop(0, L, plain, (ghost, zero), unroll=16)
+        unused_y, q_pack = lax.fori_loop(0, L, plain, (ghost, zero), unroll=32)
         if not last:
             for side in range(2):
                 for r in range(2):
@@ -524,7 +523,7 @@
         fs=V(*level), pp=V(L + 2, I, J), zz=V(*level), qs=V(*level),
         am=V(*level), im=V(*level), gm=V(*level), gf=V(*level), gl=V(*level),
         aa=V(*level), bb=V(*level),
-        xs0=V(2, 3 * L, J), ys0=V(2, I, J), xr0=V(2, 3 * L, J), yr0=V(2, 2, I, J),
+        xs0=V(2, 3 * L, J), ys0=V(2, I, J), xr0=V(2, 3 * L, J), yr0=V(2, I, J),
         xs=V(S - 1, 2, 2 * L, J), ys=V(S - 1, I, J),
         xr=V(S - 1, 2, 2 * L, J), yr=V(S - 1, 2, I, J),
         xsa=V(2, 4 * L, J), ysa=V(2, I, J), xra=V(2, 4 * L, J), yra=V(2, 2, I, J),

time: 33.6 us -> 33.1 us (0.985)
  Pallas kernels: 32.8 us -> 32.3 us
    pallas_call x1, Pallas kernels: 31.5 us -> 31 us  [body(): pl.pallas_call(functools.partial(kernel, tuple(scratch)), out_shape=(V(*l...]
where the time goes in v5:
time: 33.1 us; the launch traced here: 33 us
  Pallas kernels  32.3 us (98%)
  between operations  0.64 us (2%)
    pallas_call x1, Pallas kernels, body(): pl.pallas_call(functools.partial(kernel, tuple(scratch)), out_shape=(V(*l...  31 us
    pallas_call x1, Pallas kernels, body(): pl.pallas_call(store_kernel, out_shape=(field,) * 4, in_specs=[vmem_spec]...  1.35 us

profile of v5, /device:TPU:1, one launch (start us, length us, event | category | flops | bytes accessed | tf_op | source)
XLA Modules:
  0.0 33.0 jit_solution(2952925199189606817)
XLA Ops:
  0.6 31.0 %shard_map.102 = (f32[32,32,128]{2,1,0:T(8,128)S(1)}, f32[32,32,128]{2,1,0:T(8,128)S(1)}, f32[32,32,128]{2,1,0:T(8,128)S(1)}, f32[32,32,128]{2,1,0:T(8,128)S(1)}) custom-call(f32[32,32,128]{2,1,0:T(8,128)} %zon.1, f32[32,32,128]{2,1,0:T(8,128)} %mer.1, f32[32,32,128]{2,1,0:T(8,128)} %ver.1, f32[32,32,128]{2,1,0:T(8,128)} %pre.1, f32[32,32,128]{2,1,0:T(8,128)} %cou.1, ...), custom_call_target="tpu_custom_call" | custom-call | tf_op jit(solution)/shard_map/pallas_call | solution.py:544
  31.6 1.3 %shard_map.103 = (f32[32,32,128]{2,1,0:T(8,128)}, f32[32,32,128]{2,1,0:T(8,128)}, f32[32,32,128]{2,1,0:T(8,128)}, f32[32,32,128]{2,1,0:T(8,128)}) custom-call(f32[32,32,128]{2,1,0:T(8,128)S(1)} %get-tuple-element.8.refs_0_, f32[32,32,128]{2,1,0:T(8,128)S(1)} %get-tuple-element.9.refs_1_, f32[32,32,128]{2,1,0:T(8,128)S(1)} %get-tuple-element.10.refs_2_, ...), custom_call_target="tpu_custom_call" | custom-call | tf_op jit(solution)/shard_map/pallas_call | solution.py:552
